TPU v7x, 32 devices: a whole 2x2x4 slice. The times are simulated.
32 devices in a mesh: prow: 8 (over z, x), pcol: 4 (over y, core).
Axes of the slice: x: 2, y: 2, z: 4, core: 2. Of those that a mesh axis runs over, the one named last changes fastest.
Arguments:
- a_matrix: bfloat16 [32768, 512], P('prow', 'pcol'), may hold values from -6 to 6
- l_panel: bfloat16 [32768, 256], P('prow', 'pcol'), may hold values from -0.375 to 0.375
- l_inverse: bfloat16 [256, 256], replicated, may hold values from -1 to 1
- pivots: int32 [256], replicated, may hold values from 0 to 32767, as said below
Outputs:
- updated: bfloat16 [32768, 512], P('prow', 'pcol')
Inputs may be any that keep to these rules, and one draw needn't show every extreme that they name: pivots[j] >= j for every j.
All inputs are finite; a program needn't handle non-finite values.
Results may differ from a plain program's by a relative error of at most 0.0039.
Values may be sent and summed in bfloat16 or wider, within the bound.
A program may use at most 64 MiB of HBM per device.

v0:
```python
import jax
import jax.numpy as jnp
from jax import lax
from jax.sharding import PartitionSpec as P


def swap_plan(pivots, panel_width):
    slot_ids = jnp.arange(panel_width, dtype=jnp.int32)
    earlier = slot_ids[None, :] < slot_ids[:, None]
    hits = (pivots[None, :] == slot_ids[:, None]) & earlier
    pointer = jnp.max(jnp.where(hits, slot_ids[None, :], -1), axis=1)
    chain = jnp.where(pointer >= 0, pointer, slot_ids)
    for _ in range(panel_width.bit_length()):
        chain = jnp.take(chain, chain)
    same = pivots[None, :] == pivots[:, None]
    previous = jnp.max(jnp.where(same & earlier, slot_ids[None, :], -1), axis=1)
    top_source = jnp.where(previous >= 0, jnp.take(chain, jnp.maximum(previous, 0)), pivots)
    later = slot_ids[None, :] > slot_ids[:, None]
    is_last = jnp.logical_not(jnp.any(same & later, axis=1))
    return (top_source, chain, is_last)


def body(a_matrix, l_panel, l_inverse, pivots):
    local_count, col_count = a_matrix.shape
    panel_width = l_inverse.shape[0]
    prow_count = lax.axis_size("prow")
    prow_index = lax.axis_index("prow")
    top_source, moved_source, is_last = swap_plan(pivots, panel_width)
    local_rows = jnp.arange(local_count, dtype=jnp.int32)
    global_rows = (
        local_rows // panel_width * prow_count + prow_index
    ) * panel_width + local_rows % panel_width

    def owner_of(wanted):
        return wanted // panel_width % prow_count

    def local_of(wanted):
        return wanted // (panel_width * prow_count) * panel_width + wanted % panel_width

    def owned_part(wanted, usable):
        taken = jnp.take(a_matrix, local_of(wanted), axis=0).astype(jnp.float32)
        return jnp.where(
            ((owner_of(wanted) == prow_index) & usable)[:, None], taken, jnp.zeros((), jnp.float32)
        )

    usable_moves = is_last & (pivots >= panel_width)
    top_part = owned_part(top_source, jnp.ones((panel_width,), jnp.bool_))
    moved_part = owned_part(moved_source, usable_moves)
    moved_rows = lax.psum(moved_part, "prow")
    landing = jnp.where(
        usable_moves & (owner_of(pivots) == prow_index), local_of(pivots), local_count
    )
    swapped = a_matrix.at[landing].set(moved_rows.astype(jnp.bfloat16), mode="drop")
    top_rows = lax.psum(top_part, "prow")
    u_block = jnp.dot(
        l_inverse, top_rows.astype(jnp.bfloat16), preferred_element_type=jnp.float32
    ).astype(jnp.bfloat16)
    panel_full = lax.all_gather(l_panel, "pcol", axis=1, tiled=True)
    update = jnp.dot(panel_full, u_block, preferred_element_type=jnp.float32)
    updated = (swapped.astype(jnp.float32) - update).astype(jnp.bfloat16)
    u_padded = jnp.concatenate(
        [u_block, jnp.zeros((local_count - panel_width, col_count), jnp.bfloat16)], axis=0
    )
    return jnp.where((global_rows < panel_width)[:, None], u_padded, updated)


def solution(mesh):
    in_specs = (P("prow", "pcol"), P("prow", "pcol"), P(), P())
    out_specs = P("prow", "pcol")
    return jax.shard_map(body, mesh=mesh, in_specs=in_specs, out_specs=out_specs, check_vma=False)
```

profile of v0, /device:TPU:0, one launch (start us, length us, event | category | flops | bytes accessed | tf_op | source)
XLA Modules:
  0.0 115.9 jit_solution(2225911435671411788)
XLA Ops:
  7.4 0.0 copy-start
  7.4 0.0 all-reduce.4.cloned.1.call-start
  7.4 1.3 %copy.16 = bf16[4096,128]{1,0:T(8,128)(2,1)S(1)} copy(bf16[4096,128]{1,0:T(8,128)(2,1)} %param.8) | data formatting | bytes 2097152
  8.6 0.0 copy-done.1
  8.6 0.2 select_reduce_fusion
  8.9 0.2 fusion.4
  9.1 1.9 %gather_fusion = s32[256]{0:T(256)S(1)} fusion(s32[256]{0:T(256)S(1)} %get-tuple-element.34, s32[1024]{0:T(1024)S(1)} %pad_clamp_fusion.11), kind=kCustom, calls=%fused_computation.clone | custom fusion | bytes 3072 | tf_op jit(solution)/shard_map/jit(_take)/gather | solution.py:14
  11.0 1.9 %gather_fusion.1 = s32[256]{0:T(256)S(1)} fusion(s32[256]{0:T(256)S(1)} %get-tuple-element.32, s32[1024]{0:T(1024)S(1)} %pad_clamp_fusion.10), kind=kCustom, calls=%fused_computation.2.clone | custom fusion | bytes 3072 | tf_op jit(solution)/shard_map/jit(_take)/gather | solution.py:14
  13.0 1.9 %gather_fusion.2 = s32[256]{0:T(256)S(1)} fusion(s32[256]{0:T(256)S(1)} %get-tuple-element.30, s32[1024]{0:T(1024)S(1)} %pad_clamp_fusion.9), kind=kCustom, calls=%fused_computation.3.clone | custom fusion | bytes 3072 | tf_op jit(solution)/shard_map/jit(_take)/gather | solution.py:14
  15.0 1.9 %gather_fusion.3 = s32[256]{0:T(256)S(1)} fusion(s32[256]{0:T(256)S(1)} %get-tuple-element.28, s32[1024]{0:T(1024)S(1)} %pad_clamp_fusion.8), kind=kCustom, calls=%fused_computation.4.clone | custom fusion | bytes 3072 | tf_op jit(solution)/shard_map/jit(_take)/gather | solution.py:14
  17.0 1.9 %gather_fusion.4 = s32[256]{0:T(256)S(1)} fusion(s32[256]{0:T(256)S(1)} %get-tuple-element.26, s32[1024]{0:T(1024)S(1)} %pad_clamp_fusion.7), kind=kCustom, calls=%fused_computation.5.clone | custom fusion | bytes 3072 | tf_op jit(solution)/shard_map/jit(_take)/gather | solution.py:14
  19.0 1.9 %gather_fusion.5 = s32[256]{0:T(256)S(1)} fusion(s32[256]{0:T(256)S(1)} %get-tuple-element.24, s32[1024]{0:T(1024)S(1)} %pad_clamp_fusion.6), kind=kCustom, calls=%fused_computation.6.clone | custom fusion | bytes 3072 | tf_op jit(solution)/shard_map/jit(_take)/gather | solution.py:14
  21.0 1.9 %gather_fusion.6 = s32[256]{0:T(256)S(1)} fusion(s32[256]{0:T(256)S(1)} %get-tuple-element.22, s32[1024]{0:T(1024)S(1)} %pad_clamp_fusion.5), kind=kCustom, calls=%fused_computation.7.clone | custom fusion | bytes 3072 | tf_op jit(solution)/shard_map/jit(_take)/gather | solution.py:14
  23.0 1.9 %gather_fusion.7 = s32[256]{0:T(256)S(1)} fusion(s32[256]{0:T(256)S(1)} %get-tuple-element.20, s32[1024]{0:T(1024)S(1)} %pad_clamp_fusion.4), kind=kCustom, calls=%fused_computation.8.clone | custom fusion | bytes 3072 | tf_op jit(solution)/shard_map/jit(_take)/gather | solution.py:14
  25.0 1.9 %gather_fusion.8 = s32[256]{0:T(256)S(1)} fusion(s32[256]{0:T(256)S(1)} %get-tuple-element.18, s32[1024]{0:T(1024)S(1)} %pad_clamp_fusion.3), kind=kCustom, calls=%fused_computation.9.clone | custom fusion | bytes 3072 | tf_op jit(solution)/shard_map/jit(_take)/gather | solution.py:14
  27.0 0.9 gather_fusion.11
  27.8 0.8 convert_select_fusion
  28.6 0.0 all-reduce.4.cloned.1.call-update
  28.6 0.0 all-gather.2.cloned.1.call-start
  28.7 0.5 all-gather.2.cloned.1.call-update
  29.2 1.9 %gather_fusion.9 = s32[256]{0:T(256)S(1)} fusion(s32[256]{0:T(256)S(1)} %get-tuple-element.10, s32[1024]{0:T(1024)S(1)} %pad_clamp_fusion.2), kind=kCustom, calls=%fused_computation.10.clone | custom fusion | bytes 3072 | tf_op jit(solution)/shard_map/jit(_take)/gather | solution.py:17
  31.3 0.9 gather_fusion.10
  32.1 0.1 convert_select_fusion.1
  32.3 40.3 %all-reduce.5 = bf16[256,128]{1,0:T(8,128)(2,1)S(1)} all-reduce(f32[256,128]{1,0:T(8,128)S(1)} %convert_select_fusion.1), channel_id=1, replica_groups=mesh['prow'=8,'pcol'=4] {'prow'}, use_global_device_ids=true, to_apply=%region_2.5 | all-reduce | flops 32768 | bytes 196608 | tf_op jit(solution)/shard_map/psum | solution.py:54
  72.6 0.0 copy-done
  72.6 0.2 convolution_convert_fusion
  72.8 29.3 %all-reduce.4.cloned.1.call-done = f32[256,128]{1,0:T(8,128)} async-done(((f32[256,128]{1,0:T(8,128)}), f32[256,128]{1,0:T(8,128)}) %all-reduce.4.cloned.1.call-update) | async-done | bytes 131088 | tf_op jit(solution)/shard_map/psum | solution.py:49
  102.1 2.2 %scatter_custom_fusion = bf16[4096,128]{1,0:T(8,128)(2,1)S(1)} fusion(bf16[4096,128]{1,0:T(8,128)(2,1)S(1)} %copy.16, s32[256]{0:T(256)S(1)} %compare_select_fusion.11, f32[256,128]{1,0:T(8,128)} %all-reduce.4.cloned.1.call-done), kind=kCustom, calls=%fused_computation.29 | custom fusion | flops 32768 | bytes 1179648 | tf_op jit(solution)/shard_map/scatter | solution.py:53
  104.3 0.5 copy.9
  104.8 0.0 all-gather.2.cloned.1.call-done
  104.9 2.2 %fusion.2 = bf16[4096,128]{0,1:T(8,128)(2,1)S(1)} fusion(bf16[128,256]{1,0:T(8,128)(2,1)S(1)} %convolution_convert_fusion, bf16[4096,256]{0,1:T(8,128)(2,1)} %all-gather.2.cloned.1.call-done, bf16[4096,128]{0,1:T(8,128)(2,1)S(1)} %copy.9, bf16[256,128]{0,1:T(8,128)(2,1)S(1)} %bitcast.13, pred[4096]{0:T(1024)(128)(4,1)S(1)} %fusion.18), kind=kOutput, calls=%fused_computation.16 | convolution fusion | flops 270532608 | bytes 4329472 | tf_op jit(solution)/shard_map/dot_general | solution.py:59
  107.1 1.3 %copy.10 = bf16[4096,128]{1,0:T(8,128)(2,1)} copy(bf16[4096,128]{0,1:T(8,128)(2,1)S(1)} %fusion.2) | data formatting | bytes 2097152 | tf_op jit(solution)/shard_map/jit(_where)/select_n | solution.py:64
  (28 shorter events, 0.3 us)
Async XLA Ops:
  7.4 65.2 %copy-start = (bf16[256,256]{1,0:T(8,128)(2,1)S(1)}, bf16[256,256]{1,0:T(8,128)(2,1)}, u32[]{:S(2)}) copy-start(bf16[256,256]{1,0:T(8,128)(2,1)} %param.10) | copy-start | bytes 393220
  7.4 1.3 %copy-start.1 = (s32[256]{0:T(256)S(1)}, s32[256]{0:T(256)}, u32[]{:S(2)}) copy-start(s32[256]{0:T(256)} %param.11) | copy-start | bytes 3076
  7.4 94.8 %all-reduce.4.cloned.1.call-start = ((), (), s32[]{:S(2)}) async-start(), calls=%async_computation | async-start | bytes 262144 | tf_op jit(solution)/shard_map/psum | solution.py:49
  28.6 76.2 %all-gather.2.cloned.1.call-start = ((), (), s32[]{:S(2)}) async-start(), calls=%async_computation.1 | async-start | bytes 2621440 | tf_op jit(solution)/shard_map/all_gather | solution.py:58
Sparse Core Ops, SparseCore 0:
  28.8 73.3 all-reduce.3
Sparse Core Ops, SparseCore 1:
  30.7 25.1 all-gather.1
where the time goes:
time: 116 us
  blocking collectives  40.3 us (35%)
  waiting for transfers between devices  29.9 us (26%)
  local copies, waits for them, and re-layouts  24.3 us (21%)
  between operations  15.2 us (13%)
  other arithmetic  3.71 us (3%)
  matrix products  2.41 us (2%)
    psum x1, blocking collectives, body(): top_rows = lax.psum(top_part, 'prow')  40.3 us
    psum x1, waiting for transfers between devices, body(): moved_rows = lax.psum(moved_part, 'prow')  29.3 us
    gather x9, local copies, waits for them, and re-layouts, swap_plan(): chain = jnp.take(chain, chain)  17.6 us
  transfers between devices with their start and end apart: 2, of which 1 were waited for; matrix products, arithmetic and copies ran while one was open for 5% of the time, Pallas kernels for 0%

commit v1 on v0

--- a/solution.py
+++ b/solution.py
@@ -1,7 +1,16 @@
+import functools
 import jax
 import jax.numpy as jnp
 from jax import lax
 from jax.sharding import PartitionSpec as P
+
+
+def block_order(w_in, a_name):
+    y = lax.all_gather(w_in, axis_name=a_name)
+    return jnp.sum(y, axis=0)
+
+
+cells_work = functools.partial(block_order, a_name="prow")
 
 
 def swap_plan(pivots, panel_width):
@@ -51,7 +60,7 @@
         usable_moves & (owner_of(pivots) == prow_index), local_of(pivots), local_count
     )
     swapped = a_matrix.at[landing].set(moved_rows.astype(jnp.bfloat16), mode="drop")
-    top_rows = lax.psum(top_part, "prow")
+    top_rows = cells_work(top_part)
     u_block = jnp.dot(
         l_inverse, top_rows.astype(jnp.bfloat16), preferred_element_type=jnp.float32
     ).astype(jnp.bfloat16)

time: 116 us -> 176 us (1.52)
  waiting for transfers between devices: 29.9 us -> 130 us
  blocking collectives: 40.3 us -> 0 us
  other arithmetic: 3.71 us -> 5.67 us
  between operations: 15.2 us -> 13.4 us
    psum x1 -> x0, blocking collectives: 40.3 us -> none  [body(): top_rows = lax.psum(top_part, 'prow')]
    psum x1, waiting for transfers between devices: 29.3 us -> 68.9 us  [body(): moved_rows = lax.psum(moved_part, 'prow')]
    all_gather x0 -> x1, waiting for transfers between devices: none -> 38.8 us  [block_order(): y = lax.all_gather(w_in, axis_name=a_name)]
    all_gather x1, waiting for transfers between devices: 0.03 us -> 21.4 us  [body(): panel_full = lax.all_gather(l_panel, 'pcol', axis=1, tiled=True)]
  transfers between devices with their start and end apart: 2 -> 3, of which waited for: 1 -> 3; matrix products, arithmetic and copies ran while one was open for 5% -> 4% of each run, Pallas kernels for 0% -> 0%
where the time goes in v1:
time: 176 us
  waiting for transfers between devices  130 us (74%)
  local copies, waits for them, and re-layouts  24.3 us (14%)
  between operations  13.4 us (8%)
  other arithmetic  5.67 us (3%)
  matrix products  2.35 us (1%)
    psum x1, waiting for transfers between devices, body(): moved_rows = lax.psum(moved_part, 'prow')  68.9 us
    all_gather x1, waiting for transfers between devices, block_order(): y = lax.all_gather(w_in, axis_name=a_name)  38.8 us
    all_gather x1, waiting for transfers between devices, body(): panel_full = lax.all_gather(l_panel, 'pcol', axis=1, tiled=True)  21.4 us
    gather x9, local copies, waits for them, and re-layouts, swap_plan(): chain = jnp.take(chain, chain)  17.5 us
  transfers between devices with their start and end apart: 3, of which 3 were waited for; matrix products, arithmetic and copies ran while one was open for 4% of the time, Pallas kernels for 0%

profile of v1, /device:TPU:0, one launch (start us, length us, event | category | flops | bytes accessed | tf_op | source)
XLA Modules:
  0.0 175.6 jit_solution(107831242290496003)
XLA Ops:
  6.5 0.0 copy-start
  6.5 1.3 copy.14
  7.8 0.2 select_reduce_fusion
  8.0 0.2 fusion.4
  8.2 1.9 %gather_fusion = s32[256]{0:T(256)S(1)} fusion(s32[256]{0:T(256)S(1)} %get-tuple-element.34, s32[1024]{0:T(1024)S(1)} %pad_clamp_fusion.11), kind=kCustom, calls=%fused_computation.clone | custom fusion | bytes 3072 | tf_op jit(solution)/shard_map/jit(_take)/gather | solution.py:23
  10.2 1.9 %gather_fusion.1 = s32[256]{0:T(256)S(1)} fusion(s32[256]{0:T(256)S(1)} %get-tuple-element.32, s32[1024]{0:T(1024)S(1)} %pad_clamp_fusion.10), kind=kCustom, calls=%fused_computation.2.clone | custom fusion | bytes 3072 | tf_op jit(solution)/shard_map/jit(_take)/gather | solution.py:23
  12.2 1.9 %gather_fusion.2 = s32[256]{0:T(256)S(1)} fusion(s32[256]{0:T(256)S(1)} %get-tuple-element.30, s32[1024]{0:T(1024)S(1)} %pad_clamp_fusion.9), kind=kCustom, calls=%fused_computation.3.clone | custom fusion | bytes 3072 | tf_op jit(solution)/shard_map/jit(_take)/gather | solution.py:23
  14.2 1.9 %gather_fusion.3 = s32[256]{0:T(256)S(1)} fusion(s32[256]{0:T(256)S(1)} %get-tuple-element.28, s32[1024]{0:T(1024)S(1)} %pad_clamp_fusion.8), kind=kCustom, calls=%fused_computation.4.clone | custom fusion | bytes 3072 | tf_op jit(solution)/shard_map/jit(_take)/gather | solution.py:23
  16.1 1.9 %gather_fusion.4 = s32[256]{0:T(256)S(1)} fusion(s32[256]{0:T(256)S(1)} %get-tuple-element.26, s32[1024]{0:T(1024)S(1)} %pad_clamp_fusion.7), kind=kCustom, calls=%fused_computation.5.clone | custom fusion | bytes 3072 | tf_op jit(solution)/shard_map/jit(_take)/gather | solution.py:23
  18.1 1.9 %gather_fusion.5 = s32[256]{0:T(256)S(1)} fusion(s32[256]{0:T(256)S(1)} %get-tuple-element.24, s32[1024]{0:T(1024)S(1)} %pad_clamp_fusion.6), kind=kCustom, calls=%fused_computation.6.clone | custom fusion | bytes 3072 | tf_op jit(solution)/shard_map/jit(_take)/gather | solution.py:23
  20.1 1.9 %gather_fusion.6 = s32[256]{0:T(256)S(1)} fusion(s32[256]{0:T(256)S(1)} %get-tuple-element.22, s32[1024]{0:T(1024)S(1)} %pad_clamp_fusion.5), kind=kCustom, calls=%fused_computation.7.clone | custom fusion | bytes 3072 | tf_op jit(solution)/shard_map/jit(_take)/gather | solution.py:23
  22.1 1.9 %gather_fusion.7 = s32[256]{0:T(256)S(1)} fusion(s32[256]{0:T(256)S(1)} %get-tuple-element.20, s32[1024]{0:T(1024)S(1)} %pad_clamp_fusion.4), kind=kCustom, calls=%fused_computation.8.clone | custom fusion | bytes 3072 | tf_op jit(solution)/shard_map/jit(_take)/gather | solution.py:23
  24.1 1.9 %gather_fusion.8 = s32[256]{0:T(256)S(1)} fusion(s32[256]{0:T(256)S(1)} %get-tuple-element.18, s32[1024]{0:T(1024)S(1)} %pad_clamp_fusion.3), kind=kCustom, calls=%fused_computation.9.clone | custom fusion | bytes 3072 | tf_op jit(solution)/shard_map/jit(_take)/gather | solution.py:23
  26.1 0.9 gather_fusion.11
  26.9 0.8 convert_select_fusion
  27.7 0.0 all-reduce.3.cloned.1.call-update
  27.8 0.0 all-gather.6.cloned.1.call-start
  27.8 1.9 %gather_fusion.9 = s32[256]{0:T(256)S(1)} fusion(s32[256]{0:T(256)S(1)} %get-tuple-element.10, s32[1024]{0:T(1024)S(1)} %pad_clamp_fusion.2), kind=kCustom, calls=%fused_computation.10.clone | custom fusion | bytes 3072 | tf_op jit(solution)/shard_map/jit(_take)/gather | solution.py:26
  29.8 0.9 gather_fusion.10
  30.7 0.8 convert_select_fusion.1
  31.5 0.0 all-gather.6.cloned.1.call-update
  31.5 0.0 all-gather.4.cloned.1.call-start
  31.6 0.7 all-gather.4.cloned.1.call-update
  32.3 68.9 %all-reduce.3.cloned.1.call-done = f32[256,128]{1,0:T(8,128)} async-done(((f32[256,128]{1,0:T(8,128)}), f32[256,128]{1,0:T(8,128)}) %all-reduce.3.cloned.1.call-update) | async-done | bytes 131088 | tf_op jit(solution)/shard_map/psum | solution.py:58
  101.2 2.2 %scatter_custom_fusion = bf16[4096,128]{1,0:T(8,128)(2,1)S(1)} fusion(bf16[4096,128]{1,0:T(8,128)(2,1)S(1)} %copy.14, s32[256]{0:T(256)S(1)} %compare_select_fusion.11, f32[256,128]{1,0:T(8,128)} %all-reduce.3.cloned.1.call-done), kind=kCustom, calls=%fused_computation.29 | custom fusion | flops 32768 | bytes 1179648 | tf_op jit(solution)/shard_map/scatter | solution.py:62
  103.3 0.5 copy.9
  103.9 38.8 %all-gather.6.cloned.1.call-done = f32[2048,128]{1,0:T(8,128)} async-done(((f32[256,128]{1,0:T(8,128)}), f32[2048,128]{1,0:T(8,128)}) %all-gather.6.cloned.1.call-update) | async-done | bytes 1048592 | tf_op jit(solution)/shard_map/all_gather | solution.py:9
  142.7 1.3 reduce_sum.9
  144.0 0.2 convolution_convert_fusion
  144.2 21.4 %all-gather.4.cloned.1.call-done = bf16[4096,256]{0,1:T(8,128)(2,1)} async-done(((bf16[4096,64]{0,1:T(8,128)(2,1)}), bf16[4096,256]{0,1:T(8,128)(2,1)}) %all-gather.4.cloned.1.call-update) | async-done | bytes 2097168 | tf_op jit(solution)/shard_map/all_gather | solution.py:67
  165.6 2.2 %fusion.2 = bf16[4096,128]{0,1:T(8,128)(2,1)S(1)} fusion(bf16[128,256]{1,0:T(8,128)(2,1)S(1)} %convolution_convert_fusion, bf16[4096,256]{0,1:T(8,128)(2,1)} %all-gather.4.cloned.1.call-done, bf16[4096,128]{0,1:T(8,128)(2,1)S(1)} %copy.9, bf16[256,128]{0,1:T(8,128)(2,1)S(1)} %bitcast.15, pred[4096]{0:T(1024)(128)(4,1)S(1)} %fusion.18), kind=kOutput, calls=%fused_computation.16 | convolution fusion | flops 270532608 | bytes 4329472 | tf_op jit(solution)/shard_map/dot_general | solution.py:68
  167.7 1.3 copy.10
  (31 shorter events, 0.3 us)
Async XLA Ops:
  6.5 137.4 %copy-start = (bf16[256,256]{1,0:T(8,128)(2,1)S(1)}, bf16[256,256]{1,0:T(8,128)(2,1)}, u32[]{:S(2)}) copy-start(bf16[256,256]{1,0:T(8,128)(2,1)} %param.10) | copy-start | bytes 393220
  6.5 1.3 copy-start.1
  6.5 94.6 %all-reduce.3.cloned.1.call-start = ((), (), s32[]{:S(2)}) async-start(), calls=%async_computation | async-start | bytes 262144 | tf_op jit(solution)/shard_map/psum | solution.py:58
  27.8 114.9 %all-gather.6.cloned.1.call-start = ((), (), s32[]{:S(2)}) async-start(), calls=%async_computation.2 | async-start | bytes 1179648 | tf_op jit(solution)/shard_map/all_gather | solution.py:9
  31.5 134.0 %all-gather.4.cloned.1.call-start = ((), (), s32[]{:S(2)}) async-start(), calls=%async_computation.1 | async-start | bytes 2621440 | tf_op jit(solution)/shard_map/all_gather | solution.py:67
Sparse Core Ops, SparseCore 0:
  27.9 73.2 all-reduce.2
  103.3 39.3 all-gather.5
  144.3 21.2 all-gather.3
